TPU v7x, 32 devices: a whole 2x2x4 slice. The times are simulated.
32 devices in a mesh: sp: 16 (over z, x, core), dp: 2 (over y).
Axes of the slice: x: 2, y: 2, z: 4, core: 2. Of those that a mesh axis runs over, the one named last changes fastest.
Arguments:
- queries: bfloat16 [1536, 24, 128], P(('dp', 'sp')), parts along dimension 0, may hold values from -12 to 12
- keys: bfloat16 [1536, 24, 128], P(('dp', 'sp')), parts along dimension 0, may hold values from -6 to 6
- values: bfloat16 [1536, 24, 128], P(('dp', 'sp')), parts along dimension 0, may hold values from -6 to 6
Outputs:
- attended: bfloat16 [1536, 3072], P(('dp', 'sp')), parts along dimension 0
There are 2 independent parts, one for each index of `dp`. A program takes and returns all parts, laid end to end along the dimension named above; each array names one. Nothing has to cross between parts.
All inputs are finite; a program needn't handle non-finite values.
Results may differ from a plain program's by a relative error of at most 0.0049.
Values may be sent and summed in bfloat16 or wider, within the bound.
A program may use at most 64 MiB of HBM per device.

v0:
```python
import jax
import jax.numpy as jnp
from jax import lax
from jax.sharding import PartitionSpec as P

HGROUPS = 8


def attend(triple):
    head_q, head_k, head_v = triple
    scale = 1.0 / head_q.shape[-1] ** 0.5
    scores = jnp.dot(head_q, head_k.T, preferred_element_type=jnp.float32) * scale
    weights = jax.nn.softmax(scores, axis=-1).astype(jnp.bfloat16)
    return jnp.dot(weights, head_v, preferred_element_type=jnp.float32)


def to_owners(field, groups, blocks):
    tokens = field.shape[0]
    feat = field.shape[1] * field.shape[2] // groups
    shaped = field.reshape(blocks, tokens // blocks, groups, feat)
    shaped = shaped.transpose(2, 0, 1, 3)
    return shaped.reshape(groups * blocks, tokens // blocks, feat)


def to_copies(field, groups, blocks):
    tokens = field.shape[0]
    feat = field.shape[1] * field.shape[2] // groups
    shaped = field.reshape(tokens, groups, feat).transpose(1, 0, 2)
    copies = jnp.broadcast_to(shaped[:, None], (groups, blocks, tokens, feat))
    return copies.reshape(groups * blocks, tokens, feat)


def from_owners(received, groups, blocks):
    rows = received.shape[1]
    feat = received.shape[2]
    shaped = received.reshape(groups, blocks, rows, feat).transpose(1, 2, 0, 3)
    return shaped.reshape(blocks * rows, groups * feat)


def shards(queries, keys, values):
    tokens, heads, width = queries.shape
    groups = HGROUPS
    blocks = lax.axis_size("sp") // groups
    per_group = heads // groups
    send_q = to_owners(queries, groups, blocks)
    send_k = to_copies(keys, groups, blocks)
    send_v = to_copies(values, groups, blocks)
    got_q = lax.all_to_all(send_q, "sp", split_axis=0, concat_axis=0, tiled=True)
    got_k = lax.all_to_all(send_k, "sp", split_axis=0, concat_axis=0, tiled=True)
    got_v = lax.all_to_all(send_v, "sp", split_axis=0, concat_axis=0, tiled=True)
    local_q = got_q.reshape(-1, per_group, width).transpose(1, 0, 2)
    local_k = got_k.reshape(-1, per_group, width).transpose(1, 0, 2)
    local_v = got_v.reshape(-1, per_group, width).transpose(1, 0, 2)
    result = lax.map(attend, (local_q, local_k, local_v))
    count = result.shape[1]
    local_out = result.transpose(1, 0, 2).reshape(count, per_group * width).astype(jnp.bfloat16)
    outgoing = local_out.reshape(groups * blocks, tokens // blocks, per_group * width)
    returned = lax.all_to_all(outgoing, "sp", split_axis=0, concat_axis=0, tiled=True)
    return from_owners(returned, groups, blocks)


def solution(mesh):
    return jax.shard_map(
        shards,
        mesh=mesh,
        in_specs=(
            P(("dp", "sp"), None, None),
            P(("dp", "sp"), None, None),
            P(("dp", "sp"), None, None),
        ),
        out_specs=P(("dp", "sp"), None),
        check_vma=False,
    )
```

profile of v0, /device:TPU:1, one launch (start us, length us, event | category | flops | bytes accessed | tf_op | source)
XLA Modules:
  0.0 80.1 jit_solution(16801572065878386620)
XLA Ops:
  0.0 0.0 copy-start
  0.0 1.1 %reshape.41 = bf16[2,24,8,384]{3,2,1,0:T(8,128)(2,1)S(1)} reshape(bf16[48,24,128]{2,1,0:T(8,128)(2,1)} %param.5) | data formatting | bytes 589824 | tf_op jit(solution)/shard_map/reshape | solution.py:20
  1.2 0.7 copy.12
  1.9 7.3 %all-to-all-start = ((bf16[16,24,384]{2,1,0:T(8,128)(2,1)}), bf16[16,24,384]{2,1,0:T(8,128)(2,1)S(1)}, u32[]{:S(2)}, u32[]{:S(2)}) async-start(bf16[16,24,384]{2,1,0:T(8,128)(2,1)} %bitcast.5), calls=%async_computation | async-start | bytes 589824 | tf_op jit(solution)/shard_map/all_to_all | solution.py:48
  9.2 0.0 copy-done
  9.2 0.1 reshape.44
  9.4 0.0 copy-start.1
  9.4 10.0 %all-to-all-done = bf16[16,24,384]{2,1,0:T(8,128)(2,1)S(1)} async-done(((bf16[16,24,384]{2,1,0:T(8,128)(2,1)}), bf16[16,24,384]{2,1,0:T(8,128)(2,1)S(1)}, u32[]{:S(2)}, u32[]{:S(2)}) %all-to-all-start) | async-done | bytes 294944 | tf_op jit(solution)/shard_map/all_to_all | solution.py:48
  19.5 0.9 %broadcast_in_dim.10 = bf16[8,2,48,384]{3,2,1,0:T(8,128)(2,1)} broadcast(bf16[8,48,384]{2,1,0:T(8,128)(2,1)S(1)} %copy.13), dimensions={0,2,3} | broadcast | bytes 884736 | tf_op jit(solution)/shard_map/broadcast_in_dim | solution.py:29
  20.3 3.8 %all-to-all-start.1 = ((bf16[16,48,384]{2,1,0:T(8,128)(2,1)}), bf16[16,48,384]{2,1,0:T(8,128)(2,1)S(1)}, u32[]{:S(2)}, u32[]{:S(2)}) async-start(bf16[16,48,384]{2,1,0:T(8,128)(2,1)} %bitcast.8), calls=%async_computation.1 | async-start | bytes 1179648 | tf_op jit(solution)/shard_map/all_to_all | solution.py:49
  24.1 0.0 copy-done.1
  24.1 0.1 reshape.47
  24.3 15.1 %all-to-all-done.1 = bf16[16,48,384]{2,1,0:T(8,128)(2,1)S(1)} async-done(((bf16[16,48,384]{2,1,0:T(8,128)(2,1)}), bf16[16,48,384]{2,1,0:T(8,128)(2,1)S(1)}, u32[]{:S(2)}, u32[]{:S(2)}) %all-to-all-start.1) | async-done | bytes 589856 | tf_op jit(solution)/shard_map/all_to_all | solution.py:49
  39.4 0.9 %broadcast_in_dim.11 = bf16[8,2,48,384]{3,2,1,0:T(8,128)(2,1)} broadcast(bf16[8,48,384]{2,1,0:T(8,128)(2,1)S(1)} %copy.14), dimensions={0,2,3} | broadcast | bytes 884736 | tf_op jit(solution)/shard_map/broadcast_in_dim | solution.py:29
  40.2 4.6 %all-to-all-start.2 = ((bf16[16,48,384]{2,1,0:T(8,128)(2,1)}), bf16[16,48,384]{2,1,0:T(8,128)(2,1)S(1)}, u32[]{:S(2)}, u32[]{:S(2)}) async-start(bf16[16,48,384]{2,1,0:T(8,128)(2,1)} %bitcast.11), calls=%async_computation.2 | async-start | bytes 1179648 | tf_op jit(solution)/shard_map/all_to_all | solution.py:50
  44.9 0.1 reshape.43
  45.0 0.2 reshape.46
  45.2 0.1 copy.16
  45.3 14.7 %all-to-all-done.2 = bf16[16,48,384]{2,1,0:T(8,128)(2,1)S(1)} async-done(((bf16[16,48,384]{2,1,0:T(8,128)(2,1)}), bf16[16,48,384]{2,1,0:T(8,128)(2,1)S(1)}, u32[]{:S(2)}, u32[]{:S(2)}) %all-to-all-start.2) | async-done | bytes 589856 | tf_op jit(solution)/shard_map/all_to_all | solution.py:50
  60.1 0.2 reshape.49
  60.3 0.1 copy.17
  60.4 3.7 %while.10 = (s32[]{:T(128)}, bf16[3,384,128]{2,1,0:T(8,128)(2,1)S(1)}, bf16[3,384,128]{2,1,0:T(8,128)(2,1)S(1)}, bf16[3,768,128]{2,1,0:T(8,128)(2,1)S(1)}, bf16[3,768,128]{2,1,0:T(8,128)(2,1)S(1)}, /*index=5*/s32[]{:T(128)}) while((s32[]{:T(128)}, bf16[3,384,128]{2,1,0:T(8,128)(2,1)S(1)}, bf16[3,384,128]{2,1,0:T(8,128)(2,1)S(1)}, ...), condition=%wide.region_3.4_spmd, body=%wide.region_0.3_spmd.sunk | while | flops 153058560 | bytes 4237893 | solution.py:54
  60.4 0.4 fusion.16
  60.8 0.4 fusion.17
  61.1 0.5 fusion.18
  61.6 0.4 fusion.16
  62.0 0.4 fusion.17
  62.4 0.5 fusion.18
  62.8 0.4 fusion.16
  63.2 0.4 fusion.17
  63.6 0.5 fusion.18
  64.1 0.3 copy.18
  64.3 0.3 convert_element_type.15
  64.6 14.7 %all_to_all.20 = bf16[16,24,384]{2,1,0:T(8,128)(2,1)S(1)} all-to-all(bf16[16,24,384]{2,1,0:T(8,128)(2,1)S(1)} %convert_element_type.15), channel_id=1, replica_groups=mesh['sp'=16,'dp'=2] {'sp'}, dimensions={0} | all-to-all | bytes 589824 | tf_op jit(solution)/shard_map/all_to_all | solution.py:58
  79.3 0.1 copy.19
  79.4 0.8 copy.20
  (4 shorter events, 0.1 us)
Async XLA Ops:
  0.0 9.2 %copy-start = (bf16[48,24,128]{2,1,0:T(8,128)(2,1)S(1)}, bf16[48,24,128]{2,1,0:T(8,128)(2,1)}, u32[]{:S(2)}) copy-start(bf16[48,24,128]{2,1,0:T(8,128)(2,1)} %param.6) | copy-start | bytes 884740
  1.9 17.6 %all-to-all-start = ((bf16[16,24,384]{2,1,0:T(8,128)(2,1)}), bf16[16,24,384]{2,1,0:T(8,128)(2,1)S(1)}, u32[]{:S(2)}, u32[]{:S(2)}) async-start(bf16[16,24,384]{2,1,0:T(8,128)(2,1)} %bitcast.5), calls=%async_computation | async-start | bytes 589824 | tf_op jit(solution)/shard_map/all_to_all | solution.py:48
  9.4 14.7 %copy-start.1 = (bf16[48,24,128]{2,1,0:T(8,128)(2,1)S(1)}, bf16[48,24,128]{2,1,0:T(8,128)(2,1)}, u32[]{:S(2)}) copy-start(bf16[48,24,128]{2,1,0:T(8,128)(2,1)} %param.7) | copy-start | bytes 884740
  20.3 19.0 %all-to-all-start.1 = ((bf16[16,48,384]{2,1,0:T(8,128)(2,1)}), bf16[16,48,384]{2,1,0:T(8,128)(2,1)S(1)}, u32[]{:S(2)}, u32[]{:S(2)}) async-start(bf16[16,48,384]{2,1,0:T(8,128)(2,1)} %bitcast.8), calls=%async_computation.1 | async-start | bytes 1179648 | tf_op jit(solution)/shard_map/all_to_all | solution.py:49
  40.2 19.8 %all-to-all-start.2 = ((bf16[16,48,384]{2,1,0:T(8,128)(2,1)}), bf16[16,48,384]{2,1,0:T(8,128)(2,1)S(1)}, u32[]{:S(2)}, u32[]{:S(2)}) async-start(bf16[16,48,384]{2,1,0:T(8,128)(2,1)} %bitcast.11), calls=%async_computation.2 | async-start | bytes 1179648 | tf_op jit(solution)/shard_map/all_to_all | solution.py:50
where the time goes:
time: 81 us; the launch traced here: 80.1 us
  waiting for transfers between devices  39.8 us (49%)
  starting transfers between devices  15.7 us (19%)
  blocking collectives  14.7 us (18%)
  local copies, waits for them, and re-layouts  6.04 us (7%)
  matrix products  2.61 us (3%)
  other arithmetic  1.05 us (1%)
    all_to_all x1, waiting for transfers between devices, shards(): lax.all_to_all(send_k, 'sp', split_axis=0, concat_axis=0, tiled=True)  15.1 us
    all_to_all x1, waiting for transfers between devices, shards(): lax.all_to_all(send_v, 'sp', split_axis=0, concat_axis=0, tiled=True)  14.7 us
    all_to_all x1, blocking collectives, shards(): lax.all_to_all(outgoing, 'sp', split_axis=0, concat_axis=0, tiled=True)  14.7 us
    all_to_all x1, waiting for transfers between devices, shards(): lax.all_to_all(send_q, 'sp', split_axis=0, concat_axis=0, tiled=True)  10 us
    all_to_all x1, starting transfers between devices, shards(): lax.all_to_all(send_q, 'sp', split_axis=0, concat_axis=0, tiled=True)  7.31 us
    all_to_all x1, starting transfers between devices, shards(): lax.all_to_all(send_v, 'sp', split_axis=0, concat_axis=0, tiled=True)  4.64 us
    all_to_all x1, starting transfers between devices, shards(): lax.all_to_all(send_k, 'sp', split_axis=0, concat_axis=0, tiled=True)  3.77 us
    broadcast_in_dim x2, local copies, waits for them, and re-layouts, to_copies(): copies = jnp.broadcast_to(shaped[:, None], (groups, blocks, tokens, feat))  1.76 us
  transfers between devices with their start and end apart: 3, of which 3 were waited for; matrix products, arithmetic and copies ran while one was open for 1% of the time, Pallas kernels for 0%

commit v1 on v0

v1 whole, which is shorter than its diff:
```python
import functools
import math

import jax
import jax.numpy as jnp
from jax import lax
from jax.experimental import pallas as pl
from jax.experimental.pallas import tpu as pltpu
from jax.sharding import PartitionSpec as P

HGROUPS = 8
MESH = pl.DeviceIdType.MESH


def order_of(group, groups):
    half = groups // 2
    side = group // half
    far = [(1 - side) * half + lax.rem(group + step, half) for step in range(half)]
    near = [side * half + lax.rem(group + step, half) for step in range(1, half)]
    return far + near


def kernel(
    groups, blocks, per_group,
    q_hbm, k_hbm, v_hbm, out_hbm,
    raw, wide, send, held, result, landed,
    in_sem, own_sem, send_sem, recv_sem, pass_sem, took_sem, back_sem, home_sem, out_sem,
):
    me = lax.axis_index("sp")
    group, block = me // blocks, lax.rem(me, blocks)
    tokens, heads, width = q_hbm.shape
    half = groups // 2
    others = order_of(group, groups)
    partners = [lax.rem(block + step, blocks) for step in range(1, blocks)]

    loads = [
        pltpu.make_async_copy(src, raw.at[i], in_sem.at[i])
        for i, src in enumerate((q_hbm, k_hbm, v_hbm))
    ]
    for load in loads:
        load.start()

    barrier = pltpu.get_barrier_semaphore()
    for other in others:
        pl.semaphore_signal(barrier, inc=1, device_id={"sp": other * blocks + block}, device_id_type=MESH)
    for partner in partners:
        pl.semaphore_signal(barrier, inc=1, device_id={"sp": group * blocks + partner}, device_id_type=MESH)

    for i, load in enumerate(loads):
        load.wait()
        wide[i] = raw[i].astype(jnp.float32).reshape(tokens * heads, width)

    def outward(j, other):
        return pltpu.make_async_remote_copy(
            src_ref=send.at[other, j],
            dst_ref=held.at[j, block, group],
            send_sem=send_sem.at[j, other],
            recv_sem=recv_sem.at[j, group],
            device_id={"sp": other * blocks + block},
            device_id_type=MESH,
        )

    def inward(j, other):
        return pltpu.make_async_remote_copy(
            src_ref=send.at[other, j],
            dst_ref=held.at[j, block, other],
            send_sem=send_sem.at[j, other],
            recv_sem=recv_sem.at[j, other],
            device_id={"sp": other * blocks + block},
            device_id_type=MESH,
        )

    def own(j):
        return pltpu.make_async_copy(send.at[group, j], held.at[j, block, group], own_sem.at[j])

    def share(j, source, partner):
        part = held.at[j, block, source, pl.ds(1, 2)]
        return pltpu.make_async_remote_copy(
            src_ref=part,
            dst_ref=part,
            send_sem=pass_sem.at[j, partner, source],
            recv_sem=took_sem.at[j, block, source],
            device_id={"sp": group * blocks + partner},
            device_id_type=MESH,
        )

    def shared(j, source, partner):
        part = held.at[j, partner, source, pl.ds(1, 2)]
        return pltpu.make_async_remote_copy(
            src_ref=part,
            dst_ref=part,
            send_sem=pass_sem.at[j, partner, source],
            recv_sem=took_sem.at[j, partner, source],
            device_id={"sp": group * blocks + partner},
            device_id_type=MESH,
        )

    def columns(of, j):
        return pl.ds(pl.multiple_of((of * per_group + j) * width, width), width)

    def back(j, other):
        return pltpu.make_async_remote_copy(
            src_ref=result.at[j, other],
            dst_ref=landed.at[:, columns(group, j)],
            send_sem=back_sem.at[j, other],
            recv_sem=home_sem.at[j, group],
            device_id={"sp": other * blocks + block},
            device_id_type=MESH,
        )

    def home(j, other):
        return pltpu.make_async_remote_copy(
            src_ref=result.at[j, other],
            dst_ref=landed.at[:, columns(other, j)],
            send_sem=back_sem.at[j, other],
            recv_sem=home_sem.at[j, other],
            device_id={"sp": other * blocks + block},
            device_id_type=MESH,
        )

    def own_back(j):
        return pltpu.make_async_copy(
            result.at[j, group], landed.at[:, columns(group, j)], home_sem.at[j, group]
        )

    for j in range(per_group):
        for to in range(groups):
            head = to * per_group + j
            for i in range(3):
                rows = wide[i, pl.ds(head, tokens, stride=heads), :]
                send[to, j, i] = rows.astype(jnp.bfloat16)
        if j == 0:
            pl.semaphore_wait(barrier, groups - 1 + blocks - 1)
        for other in others:
            outward(j, other).start()
        own(j).start()

    factor = math.log2(math.e) / math.sqrt(width)
    for j in range(per_group):
        own(j).wait()
        for partner in partners:
            share(j, group, partner).start()
        for other in others:
            inward(j, other).wait_recv()
            for partner in partners:
                share(j, other, partner).start()
        for partner in partners:
            for source in [group] + others:
                shared(j, source, partner).wait_recv()
        keys = held[j, :, :, 1].reshape(-1, width)
        values = held[j, :, :, 2].reshape(-1, width)
        side = group // half
        for first, picked in (((1 - side) * half, others[:half]), (side * half, others[half:])):
            queries = held[j, block, pl.ds(first, half), 0].reshape(half * tokens, width)
            scores = lax.dot_general(
                queries, keys, (((1,), (1,)), ((), ())), preferred_element_type=jnp.float32
            )
            top = jnp.max(scores, axis=-1, keepdims=True)
            weights = jnp.exp2((scores - top) * factor)
            total = jnp.sum(weights, axis=-1, keepdims=True)
            attended = jnp.dot(
                weights.astype(jnp.bfloat16), values, preferred_element_type=jnp.float32
            ) / total
            result[j, pl.ds(first, half)] = attended.astype(jnp.bfloat16).reshape(half, tokens, width)
            for other in picked:
                back(j, other).start()
        own_back(j).start()

    for j in range(per_group):
        own_back(j).wait()
        for other in others:
            home(j, other).wait_recv()
    store = pltpu.make_async_copy(landed, out_hbm, out_sem)
    store.start()
    for j in range(per_group):
        for other in others:
            outward(j, other).wait_send()
            back(j, other).wait_send()
        for partner in partners:
            for source in [group] + others:
                share(j, source, partner).wait_send()
    store.wait()


def shards(queries, keys, values):
    tokens, heads, width = queries.shape
    groups = HGROUPS
    blocks = lax.axis_size("sp") // groups
    per_group = heads // groups
    kind = queries.dtype
    return pl.pallas_call(
        functools.partial(kernel, groups, blocks, per_group),
        out_shape=jax.ShapeDtypeStruct((tokens, heads * width), kind),
        in_specs=[pl.BlockSpec(memory_space=pl.ANY)] * 3,
        out_specs=pl.BlockSpec(memory_space=pl.ANY),
        scratch_shapes=[
            pltpu.VMEM((3, tokens, heads, width), kind),
            pltpu.VMEM((3, tokens * heads, width), jnp.float32),
            pltpu.VMEM((groups, per_group, 3, tokens, width), kind),
            pltpu.VMEM((per_group, blocks, groups, 3, tokens, width), kind),
            pltpu.VMEM((per_group, groups, tokens, width), kind),
            pltpu.VMEM((tokens, heads * width), kind),
            pltpu.SemaphoreType.DMA((3,)),
            pltpu.SemaphoreType.DMA((per_group,)),
            pltpu.SemaphoreType.DMA((per_group, groups)),
            pltpu.SemaphoreType.DMA((per_group, groups)),
            pltpu.SemaphoreType.DMA((per_group, blocks, groups)),
            pltpu.SemaphoreType.DMA((per_group, blocks, groups)),
            pltpu.SemaphoreType.DMA((per_group, groups)),
            pltpu.SemaphoreType.DMA((per_group, groups)),
            pltpu.SemaphoreType.DMA,
        ],
        compiler_params=pltpu.CompilerParams(collective_id=0, has_side_effects=True),
    )(queries, keys, values)


def solution(mesh):
    return jax.shard_map(
        shards,
        mesh=mesh,
        in_specs=(
            P(("dp", "sp"), None, None),
            P(("dp", "sp"), None, None),
            P(("dp", "sp"), None, None),
        ),
        out_specs=P(("dp", "sp"), None),
        check_vma=False,
    )
```

time: 81 us -> 38.4 us (0.47)
  waiting for transfers between devices: 39.8 us -> 0 us
  Pallas kernels: 0 us -> 36.6 us
  starting transfers between devices: 15.7 us -> 0 us
  blocking collectives: 14.7 us -> 0 us
  local copies, waits for them, and re-layouts: 6.04 us -> 1.69 us
  matrix products: 2.61 us -> 0 us
  other arithmetic: 1.05 us -> 0 us
    all_to_all x3 -> x0, waiting for transfers between devices: 39.8 us -> none  [the longest x1 15.1 us: shards(): lax.all_to_all(send_k, 'sp', split_axis=0, concat_axis=0, tiled=True)]
    pallas_call x0 -> x1, Pallas kernels: none -> 36.6 us  [shards(): pl.pallas_call(functools.partial(kernel, groups, blocks, per_group), out_...]
    all_to_all x3 -> x0, starting transfers between devices: 15.7 us -> none  [the longest x1 7.31 us: shards(): lax.all_to_all(send_q, 'sp', split_axis=0, concat_axis=0, tiled=True)]
    all_to_all x1 -> x0, blocking collectives: 14.7 us -> none  [shards(): lax.all_to_all(outgoing, 'sp', split_axis=0, concat_axis=0, tiled=True)]
    dot_general x6 -> x0, matrix products: 2.61 us -> none  [the longest x3 1.41 us: attend(): return jnp.dot(weights, head_v, preferred_element_type=jnp.float32)]
    reshape x6 -> x0, local copies, waits for them, and re-layouts: 1.91 us -> none  [the longest x1 1.15 us: to_owners(): shaped = field.reshape(blocks, tokens // blocks, groups, feat)]
    broadcast_in_dim x2 -> x0, local copies, waits for them, and re-layouts: 1.76 us -> none  [to_copies(): copies = jnp.broadcast_to(shaped[:, None], (groups, blocks, tokens, feat))]
    reduce_sum x3 -> x0, other arithmetic: 1.05 us -> none  [attend(): weights = jax.nn.softmax(scores, axis=-1).astype(jnp.bfloat16)]
  transfers between devices with their start and end apart: 3 -> 0, of which waited for: 3 -> 0; matrix products, arithmetic and copies ran while one was open for 1% -> 0% of each run, Pallas kernels for 0% -> 0%
where the time goes in v1:
time: 38.4 us; the launch traced here: 38.3 us
  Pallas kernels  36.6 us (95%)
  local copies, waits for them, and re-layouts  1.69 us (4%)
    pallas_call x1, Pallas kernels, shards(): pl.pallas_call(functools.partial(kernel, groups, blocks, per_group), out_...  36.6 us
    unnamed x1, local copies, waits for them, and re-layouts  1.69 us

profile of v1, /device:TPU:1, one launch (start us, length us, event | category | flops | bytes accessed | tf_op | source)
XLA Modules:
  0.0 38.3 jit_solution(17268843993623595369)
XLA Ops:
  0.0 36.6 %shard_map.37 = bf16[48,3072]{1,0:T(8,128)(2,1)} custom-call(bf16[48,24,128]{2,1,0:T(8,128)(2,1)} %q_hbm.1, bf16[48,24,128]{2,1,0:T(8,128)(2,1)} %k_hbm.1, bf16[48,24,128]{2,1,0:T(8,128)(2,1)} %v_hbm.1), custom_call_target="tpu_custom_call" | custom-call | tf_op jit(solution)/shard_map/pallas_call | solution.py:191
  36.6 1.7 %copy.5 = bf16[48,3072]{1,0:T(8,128)(2,1)} copy(bf16[48,3072]{1,0:T(8,128)(2,1)} %shard_map.37) | data formatting | bytes 589824

commit v2 on v1

--- a/solution.py
+++ b/solution.py
@@ -24,7 +24,7 @@
     groups, blocks, per_group,
     q_hbm, k_hbm, v_hbm, out_hbm,
     raw, wide, send, held, result, landed,
-    in_sem, own_sem, send_sem, recv_sem, pass_sem, took_sem, back_sem, home_sem, out_sem,
+    in_sem, own_sem, send_sem, recv_sem, pass_sem, took_sem, back_sem, home_sem,
 ):
     me = lax.axis_index("sp")
     group, block = me // blocks, lax.rem(me, blocks)
@@ -170,8 +170,7 @@
         own_back(j).wait()
         for other in others:
             home(j, other).wait_recv()
-    store = pltpu.make_async_copy(landed, out_hbm, out_sem)
-    store.start()
+    out_hbm[...] = landed[...]
     for j in range(per_group):
         for other in others:
             outward(j, other).wait_send()
@@ -179,7 +178,6 @@
         for partner in partners:
             for source in [group] + others:
                 share(j, source, partner).wait_send()
-    store.wait()
 
 
 def shards(queries, keys, values):
@@ -190,9 +188,9 @@
     kind = queries.dtype
     return pl.pallas_call(
         functools.partial(kernel, groups, blocks, per_group),
-        out_shape=jax.ShapeDtypeStruct((tokens, heads * width), kind),
+        out_shape=pltpu.VMEM((tokens, heads * width), kind),
         in_specs=[pl.BlockSpec(memory_space=pl.ANY)] * 3,
-        out_specs=pl.BlockSpec(memory_space=pl.ANY),
+        out_specs=pl.BlockSpec(memory_space=pltpu.VMEM),
         scratch_shapes=[
             pltpu.VMEM((3, tokens, heads, width), kind),
             pltpu.VMEM((3, tokens * heads, width), jnp.float32),
@@ -208,7 +206,6 @@
             pltpu.SemaphoreType.DMA((per_group, blocks, groups)),
             pltpu.SemaphoreType.DMA((per_group, groups)),
             pltpu.SemaphoreType.DMA((per_group, groups)),
-            pltpu.SemaphoreType.DMA,
         ],
         compiler_params=pltpu.CompilerParams(collective_id=0, has_side_effects=True),
     )(queries, keys, values)

time: 38.4 us -> 36.8 us (0.958)
  local copies, waits for them, and re-layouts: 1.69 us -> 0.72 us
  Pallas kernels: 36.6 us -> 36 us
    unnamed x1, local copies, waits for them, and re-layouts: 1.69 us -> 0.72 us
    pallas_call x1, Pallas kernels: 36.6 us -> 36 us  [shards(): pl.pallas_call(functools.partial(kernel, groups, blocks, per_group), out_...]
where the time goes in v2:
time: 36.8 us; the launch traced here: 36.7 us
  Pallas kernels  36 us (98%)
  local copies, waits for them, and re-layouts  0.72 us (2%)
    pallas_call x1, Pallas kernels, shards(): pl.pallas_call(functools.partial(kernel, groups, blocks, per_group), out_...  36 us

profile of v2, /device:TPU:1, one launch (start us, length us, event | category | flops | bytes accessed | tf_op | source)
XLA Modules:
  0.0 36.7 jit_solution(14228669561657970267)
XLA Ops:
  0.0 36.0 %shard_map.37 = bf16[48,3072]{1,0:T(8,128)(2,1)S(1)} custom-call(bf16[48,24,128]{2,1,0:T(8,128)(2,1)} %q_hbm.1, bf16[48,24,128]{2,1,0:T(8,128)(2,1)} %k_hbm.1, bf16[48,24,128]{2,1,0:T(8,128)(2,1)} %v_hbm.1), custom_call_target="tpu_custom_call" | custom-call | tf_op jit(solution)/shard_map/pallas_call | solution.py:189
  36.0 0.7 %copy.5 = bf16[48,3072]{1,0:T(8,128)(2,1)} copy(bf16[48,3072]{1,0:T(8,128)(2,1)S(1)} %shard_map.37) | data formatting | bytes 589824

commit v3 on v2

v3 whole, which is shorter than its diff:
```python
import functools
import math

import jax
import jax.numpy as jnp
from jax import lax
from jax.experimental import pallas as pl
from jax.experimental.pallas import tpu as pltpu
from jax.sharding import PartitionSpec as P

HGROUPS = 8
MESH = pl.DeviceIdType.MESH


def order_of(group, groups):
    half = groups // 2
    side = group // half
    far = [(1 - side) * half + lax.rem(group + step, half) for step in range(half)]
    near = [side * half + lax.rem(group + step, half) for step in range(1, half)]
    return far, near


def ranked(group, groups):
    half = groups // 2
    side, place = group // half, lax.rem(group, half)
    far = [(1 - side) * half + step for step in range(half)]
    near = [side * half + step + (step + half - place) // half for step in range(half - 1)]
    return far, near


def kernel(
    groups, blocks, per_group,
    q_hbm, k_hbm, v_hbm, landed,
    raw, wide, send, held, result,
    in_sem, send_sem, recv_sem, pass_sem, took_sem, back_sem, home_sem,
):
    me = lax.axis_index("sp")
    group, block = me // blocks, lax.rem(me, blocks)
    tokens, heads, width = q_hbm.shape
    half = groups // 2
    side = group // half
    far, near = order_of(group, groups)
    partners = [lax.rem(block + step, blocks) for step in range(1, blocks)]

    loads = [
        pltpu.make_async_copy(src, raw.at[i], in_sem.at[i])
        for i, src in enumerate((q_hbm, k_hbm, v_hbm))
    ]
    for load in loads:
        load.start()

    barrier = pltpu.get_barrier_semaphore()
    for other in far + near:
        pl.semaphore_signal(barrier, inc=1, device_id={"sp": other * blocks + block}, device_id_type=MESH)
    for partner in partners:
        pl.semaphore_signal(barrier, inc=1, device_id={"sp": group * blocks + partner}, device_id_type=MESH)

    for i, load in enumerate(loads):
        load.wait()
        wide[i] = raw[i].astype(jnp.float32).reshape(tokens * heads, width)

    def outward(j, other, part):
        return pltpu.make_async_remote_copy(
            src_ref=send.at[other, j],
            dst_ref=held.at[j, block, group],
            send_sem=send_sem,
            recv_sem=recv_sem.at[j, part],
            device_id={"sp": other * blocks + block},
            device_id_type=MESH,
        )

    def own(j):
        return pltpu.make_async_copy(send.at[group, j], held.at[j, block, group], recv_sem.at[j, 0])

    def sources(part):
        return pl.ds((side if part == 0 else 1 - side) * half, half)

    def arrived(j, part):
        whole = held.at[j, block, sources(part)]
        pltpu.make_async_copy(whole, whole, recv_sem.at[j, part]).wait()

    def share(j, part, partner):
        piece = held.at[j, block, sources(part), pl.ds(1, 2)]
        return pltpu.make_async_remote_copy(
            src_ref=piece,
            dst_ref=piece,
            send_sem=pass_sem.at[partner],
            recv_sem=took_sem.at[j, block],
            device_id={"sp": group * blocks + partner},
            device_id_type=MESH,
        )

    def shared(j, partner):
        whole = held.at[j, partner, :, pl.ds(1, 2)]
        pltpu.make_async_copy(whole, whole, took_sem.at[j, partner]).wait()

    def columns(of, j):
        return pl.ds(pl.multiple_of((of * per_group + j) * width, width), width)

    def back(j, other):
        return pltpu.make_async_remote_copy(
            src_ref=result.at[j, other],
            dst_ref=landed.at[:, columns(group, j)],
            send_sem=back_sem,
            recv_sem=home_sem,
            device_id={"sp": other * blocks + block},
            device_id_type=MESH,
        )

    def own_back(j):
        return pltpu.make_async_copy(result.at[j, group], landed.at[:, columns(group, j)], home_sem)

    for j in range(per_group):
        for to in range(groups):
            head = to * per_group + j
            for i in range(3):
                rows = wide[i, pl.ds(head, tokens, stride=heads), :]
                send[to, j, i] = rows.astype(jnp.bfloat16)
        if j == 0:
            pl.semaphore_wait(barrier, groups - 1 + blocks - 1)
        for other in far:
            outward(j, other, 1).start()
        for other in near:
            outward(j, other, 0).start()
        own(j).start()

    factor = math.log2(math.e) / math.sqrt(width)
    far, near = ranked(group, groups)
    for j in range(per_group):
        for part in range(2):
            arrived(j, part)
            for partner in partners:
                share(j, part, partner).start()
        for partner in partners:
            shared(j, partner)
        keys = held[j, :, :, 1].reshape(-1, width)
        values = held[j, :, :, 2].reshape(-1, width)
        for first, picked in (((1 - side) * half, far), (side * half, near)):
            queries = held[j, block, pl.ds(first, half), 0].reshape(half * tokens, width)
            scores = lax.dot_general(
                queries, keys, (((1,), (1,)), ((), ())), preferred_element_type=jnp.float32
            )
            top = jnp.max(scores, axis=-1, keepdims=True)
            weights = jnp.exp2((scores - top) * factor)
            total = jnp.sum(weights, axis=-1, keepdims=True)
            attended = jnp.dot(
                weights.astype(jnp.bfloat16), values, preferred_element_type=jnp.float32
            ) / total
            result[j, pl.ds(first, half)] = attended.astype(jnp.bfloat16).reshape(half, tokens, width)
            for other in picked:
                back(j, other).start()
        own_back(j).start()

    sent = send.at[pl.ds(0, groups - 1)]
    pltpu.make_async_copy(sent, sent, send_sem).wait()
    for partner in partners:
        passed = held.at[:, block, :, pl.ds(1, 2)]
        pltpu.make_async_copy(passed, passed, pass_sem.at[partner]).wait()
    given = result.at[:, pl.ds(0, groups - 1)]
    pltpu.make_async_copy(given, given, back_sem).wait()
    pltpu.make_async_copy(landed, landed, home_sem).wait()


def shards(queries, keys, values):
    tokens, heads, width = queries.shape
    groups = HGROUPS
    blocks = lax.axis_size("sp") // groups
    per_group = heads // groups
    kind = queries.dtype
    return pl.pallas_call(
        functools.partial(kernel, groups, blocks, per_group),
        out_shape=pltpu.VMEM((tokens, heads * width), kind),
        in_specs=[pl.BlockSpec(memory_space=pl.ANY)] * 3,
        out_specs=pl.BlockSpec(memory_space=pltpu.VMEM),
        scratch_shapes=[
            pltpu.VMEM((3, tokens, heads, width), kind),
            pltpu.VMEM((3, tokens * heads, width), jnp.float32),
            pltpu.VMEM((groups, per_group, 3, tokens, width), kind),
            pltpu.VMEM((per_group, blocks, groups, 3, tokens, width), kind),
            pltpu.VMEM((per_group, groups, tokens, width), kind),
            pltpu.SemaphoreType.DMA((3,)),
            pltpu.SemaphoreType.DMA,
            pltpu.SemaphoreType.DMA((per_group, 2)),
            pltpu.SemaphoreType.DMA((blocks,)),
            pltpu.SemaphoreType.DMA((per_group, blocks)),
            pltpu.SemaphoreType.DMA,
            pltpu.SemaphoreType.DMA,
        ],
        compiler_params=pltpu.CompilerParams(collective_id=0, has_side_effects=True),
    )(queries, keys, values)


def solution(mesh):
    return jax.shard_map(
        shards,
        mesh=mesh,
        in_specs=(
            P(("dp", "sp"), None, None),
            P(("dp", "sp"), None, None),
            P(("dp", "sp"), None, None),
        ),
        out_specs=P(("dp", "sp"), None),
        check_vma=False,
    )
```

time: 36.8 us -> 34.8 us (0.946)
  Pallas kernels: 36 us -> 33.9 us
    pallas_call x1, Pallas kernels: 36 us -> 33.9 us  [shards(): pl.pallas_call(functools.partial(kernel, groups, blocks, per_group), out_...]
where the time goes in v3:
time: 34.8 us; the launch traced here: 34.6 us
  Pallas kernels  33.9 us (97%)
  local copies, waits for them, and re-layouts  0.72 us (2%)
    pallas_call x1, Pallas kernels, shards(): pl.pallas_call(functools.partial(kernel, groups, blocks, per_group), out_...  33.9 us
    unnamed x1, local copies, waits for them, and re-layouts  0.72 us

profile of v3, /device:TPU:1, one launch (start us, length us, event | category | flops | bytes accessed | tf_op | source)
XLA Modules:
  0.0 34.6 jit_solution(6850143714377542325)
XLA Ops:
  0.0 33.9 %shard_map.37 = bf16[48,3072]{1,0:T(8,128)(2,1)S(1)} custom-call(bf16[48,24,128]{2,1,0:T(8,128)(2,1)} %q_hbm.1, bf16[48,24,128]{2,1,0:T(8,128)(2,1)} %k_hbm.1, bf16[48,24,128]{2,1,0:T(8,128)(2,1)} %v_hbm.1), custom_call_target="tpu_custom_call" | custom-call | tf_op jit(solution)/shard_map/pallas_call | solution.py:170
  33.9 0.7 %copy.5 = bf16[48,3072]{1,0:T(8,128)(2,1)} copy(bf16[48,3072]{1,0:T(8,128)(2,1)S(1)} %shard_map.37) | data formatting | bytes 589824

commit v4 on v3

--- a/solution.py
+++ b/solution.py
@@ -135,6 +135,13 @@
             shared(j, partner)
         keys = held[j, :, :, 1].reshape(-1, width)
         values = held[j, :, :, 2].reshape(-1, width)
+        if j == per_group - 1:
+            @pl.when(side == 0)
+            def release():
+                for earlier in (1,):
+                    for other in far:
+                        back(earlier, other).start()
+
         for first, picked in (((1 - side) * half, far), (side * half, near)):
             queries = held[j, block, pl.ds(first, half), 0].reshape(half * tokens, width)
             scores = lax.dot_general(
@@ -147,8 +154,14 @@
                 weights.astype(jnp.bfloat16), values, preferred_element_type=jnp.float32
             ) / total
             result[j, pl.ds(first, half)] = attended.astype(jnp.bfloat16).reshape(half, tokens, width)
-            for other in picked:
-                back(j, other).start()
+            if picked is far and j in (1,):
+                @pl.when(side > 0)
+                def forward():
+                    for other in picked:
+                        back(j, other).start()
+            else:
+                for other in picked:
+                    back(j, other).start()
         own_back(j).start()
 
     sent = send.at[pl.ds(0, groups - 1)]

time: 34.8 us -> 34.4 us (0.989); the launches traced: 34.6 us -> 33.8 us
  Pallas kernels: 33.9 us -> 33.1 us
    pallas_call x1, Pallas kernels: 33.9 us -> 33.1 us  [shards(): pl.pallas_call(functools.partial(kernel, groups, blocks, per_group), out_...]
where the time goes in v4:
time: 34.4 us; the launch traced here: 33.8 us
  Pallas kernels  33.1 us (96%)
  local copies, waits for them, and re-layouts  0.72 us (2%)
    pallas_call x1, Pallas kernels, shards(): pl.pallas_call(functools.partial(kernel, groups, blocks, per_group), out_...  33.1 us
    unnamed x1, local copies, waits for them, and re-layouts  0.72 us

profile of v4, /device:TPU:1, one launch (start us, length us, event | category | flops | bytes accessed | tf_op | source)
XLA Modules:
  0.0 33.8 jit_solution(13147880560011908619)
XLA Ops:
  0.0 33.1 %shard_map.37 = bf16[48,3072]{1,0:T(8,128)(2,1)S(1)} custom-call(bf16[48,24,128]{2,1,0:T(8,128)(2,1)} %q_hbm.1, bf16[48,24,128]{2,1,0:T(8,128)(2,1)} %k_hbm.1, bf16[48,24,128]{2,1,0:T(8,128)(2,1)} %v_hbm.1), custom_call_target="tpu_custom_call" | custom-call | tf_op jit(solution)/shard_map/pallas_call | solution.py:183
  33.1 0.7 %copy.5 = bf16[48,3072]{1,0:T(8,128)(2,1)} copy(bf16[48,3072]{1,0:T(8,128)(2,1)S(1)} %shard_map.37) | data formatting | bytes 589824
